TPU v7x, 32 devices: a whole 2x2x4 slice. The times are simulated.
32 devices in a mesh: dp: 4 (over z), ring: 2 (over y), uly: 4 (over x, core).
Axes of the slice: x: 2, y: 2, z: 4, core: 2. Of those that a mesh axis runs over, the one named last changes fastest.
Arguments:
- y_mod: bfloat16 [4, 8192, 1536], P('dp', ('ring', 'uly'))
- pre_q: bfloat16 [4, 8192, 1536], P('dp', ('ring', 'uly'))
- pre_k: bfloat16 [4, 8192, 1536], P('dp', ('ring', 'uly'))
- inv_q: float32 [4, 8192], P('dp', ('ring', 'uly'))
- inv_k: float32 [4, 8192], P('dp', ('ring', 'uly'))
- log_sum: float32 [4, 12, 8192], P('dp', None, ('ring', 'uly'))
- attn_out: bfloat16 [4, 8192, 1536], P('dp', ('ring', 'uly'))
- gate_msa: float32 [4, 1536], P('dp')
- d_resid: bfloat16 [4, 8192, 1536], P('dp', ('ring', 'uly'))
- angles: float32 [8192, 64], P(('ring', 'uly'))
- w_q: bfloat16 [1536, 1536], replicated
- w_k: bfloat16 [1536, 1536], replicated
- w_v: bfloat16 [1536, 1536], replicated
- b_v: float32 [1536], replicated
- w_o: bfloat16 [1536, 1536], replicated
- g_q: float32 [1536], replicated
- g_k: float32 [1536], replicated
Outputs:
- output 1: bfloat16 [4, 8192, 1536], P('dp', ('ring', 'uly'))
- output 2: float32 [1536, 1536], replicated
- output 3: float32 [1536, 1536], replicated
- output 4: float32 [1536, 1536], replicated
- output 5: float32 [1536, 1536], replicated
- output 6: float32 [1536], replicated
- output 7: float32 [1536], replicated
- output 8: float32 [1536], replicated
- output 9: float32 [1536], replicated
- output 10: float32 [1536], replicated
- output 11: float32 [1536], replicated
All inputs are finite; a program needn't handle non-finite values.
Results may differ from a plain program's by a relative error of at most 0.00911088.
Values are sent between devices in bfloat16 or wider.
A program may use at most 1 GiB of HBM per device.

v0:
```python
import jax
import jax.numpy as jnp
from jax import lax
from jax.sharding import PartitionSpec as P

QUERY_BLOCK = 256
ROW_SUM_DIMS = (((0,), (0,)), ((), ()))
BY_TRANSPOSE = (((1,), (1,)), ((), ()))


def rope_turn(feats, cos_tab, sin_tab):
    pairs = feats.reshape(feats.shape[:-1] + (cos_tab.shape[-1], 2))
    even_part = pairs[..., 0]
    odd_part = pairs[..., 1]
    cos_b = cos_tab[:, None, :]
    sin_b = sin_tab[:, None, :]
    turned = jnp.stack([even_part * cos_b - odd_part * sin_b, even_part * sin_b + odd_part * cos_b], axis=-1)
    return turned.reshape(feats.shape)


def norm_rope(proj, inv_rms, gain, cos_tab, sin_tab, n_heads):
    normed = proj.astype(jnp.float32) * inv_rms[..., None] * gain
    heads_view = normed.reshape(normed.shape[:-1] + (n_heads, normed.shape[-1] // n_heads))
    return rope_turn(heads_view, cos_tab, sin_tab).astype(jnp.bfloat16)


def norm_back(d_norm, proj, inv_rms, gain):
    proj_f = proj.astype(jnp.float32)
    rms_b = inv_rms[..., None]
    d_gain = jnp.sum(d_norm * proj_f * rms_b, axis=(0, 1))
    mixed = jnp.mean(proj_f * gain * d_norm, axis=-1, keepdims=True)
    d_proj = rms_b * gain * d_norm - proj_f * rms_b ** 3 * mixed
    return d_proj.astype(jnp.bfloat16), d_gain


def attend_back(q_all, da_all, lse_all, dot_all, k_seg, v_seg, dq_acc, dk_acc, dv_acc):
    seg_len = q_all.shape[1]
    blk_len = min(seg_len, QUERY_BLOCK)
    score_scale = q_all.shape[-1] ** -0.5

    def blk_body(blk_idx, acc_state):
        dq_run, dk_run, dv_run = acc_state
        blk_start = blk_idx * blk_len
        q_blk = lax.dynamic_slice_in_dim(q_all, blk_start, blk_len, axis=1)
        da_blk = lax.dynamic_slice_in_dim(da_all, blk_start, blk_len, axis=1)
        lse_blk = lax.dynamic_slice_in_dim(lse_all, blk_start, blk_len, axis=2)
        dot_blk = lax.dynamic_slice_in_dim(dot_all, blk_start, blk_len, axis=2)
        scores = jnp.einsum('bqhd,bkhd->bhqk', q_blk, k_seg, preferred_element_type=jnp.float32) * score_scale
        p_mat = jnp.exp(scores - lse_blk[..., None])
        dv_run = dv_run + jnp.einsum('bhqk,bqhd->bkhd', p_mat.astype(jnp.bfloat16), da_blk, preferred_element_type=jnp.float32)
        dp_mat = jnp.einsum('bqhd,bkhd->bhqk', da_blk, v_seg, preferred_element_type=jnp.float32)
        ds_low = (p_mat * (dp_mat - dot_blk[..., None])).astype(jnp.bfloat16)
        dq_new = jnp.einsum('bhqk,bkhd->bqhd', ds_low, k_seg, preferred_element_type=jnp.float32) * score_scale
        dk_run = dk_run + jnp.einsum('bhqk,bqhd->bkhd', ds_low, q_blk, preferred_element_type=jnp.float32) * score_scale
        dq_old = lax.dynamic_slice_in_dim(dq_run, blk_start, blk_len, axis=1)
        dq_run = lax.dynamic_update_slice_in_dim(dq_run, dq_old + dq_new, blk_start, axis=1)
        return dq_run, dk_run, dv_run

    return lax.fori_loop(0, seg_len // blk_len, blk_body, (dq_acc, dk_acc, dv_acc))


def solution(mesh):
    ring_size = mesh.shape['ring']
    ring_perm = [(idx, (idx + 1) % ring_size) for idx in range(ring_size)]
    tok_three = P('dp', ('ring', 'uly'), None)
    tok_two = P('dp', ('ring', 'uly'))
    stat_spec = P('dp', None, ('ring', 'uly'))
    whole = P()

    def device_fn(y_mod, pre_q, pre_k, inv_q, inv_k, log_sum, attn_out, value_a8, d_resid, angles, w_q, w_k, w_v, b_v, w_o, g_q, g_k):
        n_batch, n_tok, model_width = y_mod.shape
        n_heads = log_sum.shape[1]
        head_dim = model_width // n_heads
        n_rows = n_batch * n_tok
        head_shape = (n_batch, n_tok, n_heads, head_dim)
        flat_y = y_mod.reshape(n_rows, model_width)
        d_out = (d_resid.astype(jnp.float32) * value_a8[:, None, :]).astype(jnp.bfloat16).reshape(n_rows, model_width)
        flat_attn = attn_out.reshape(n_rows, model_width)
        dw_o = lax.dot_general(flat_attn, d_out, ROW_SUM_DIMS, preferred_element_type=jnp.float32)
        db_o = jnp.sum(d_out, axis=0, dtype=jnp.float32)
        d_attn = lax.dot_general(d_out, w_o, BY_TRANSPOSE, preferred_element_type=jnp.float32).astype(jnp.bfloat16).reshape(head_shape)
        cos_tab = jnp.cos(angles)
        sin_tab = jnp.sin(angles)
        q_rot = norm_rope(pre_q, inv_q, g_q, cos_tab, sin_tab, n_heads)
        k_rot = norm_rope(pre_k, inv_k, g_k, cos_tab, sin_tab, n_heads)
        v_proj = (jnp.dot(flat_y, w_v, preferred_element_type=jnp.float32) + b_v).astype(jnp.bfloat16).reshape(head_shape)
        row_dot = jnp.einsum('bthd,bthd->bht', d_attn, attn_out.reshape(head_shape), preferred_element_type=jnp.float32)
        q_head = lax.all_to_all(q_rot, 'uly', 2, 1, tiled=True)
        k_head = lax.all_to_all(k_rot, 'uly', 2, 1, tiled=True)
        v_head = lax.all_to_all(v_proj, 'uly', 2, 1, tiled=True)
        da_head = lax.all_to_all(d_attn, 'uly', 2, 1, tiled=True)
        lse_head = lax.all_to_all(log_sum, 'uly', 1, 2, tiled=True)
        dot_head = lax.all_to_all(row_dot, 'uly', 1, 2, tiled=True)
        dq_acc = jnp.zeros(q_head.shape, jnp.float32)
        dk_cur = jnp.zeros(k_head.shape, jnp.float32)
        dv_cur = jnp.zeros(v_head.shape, jnp.float32)
        k_cur = k_head
        v_cur = v_head
        for hop_idx in range(ring_size):
            dq_acc, dk_cur, dv_cur = attend_back(q_head, da_head, lse_head, dot_head, k_cur, v_cur, dq_acc, dk_cur, dv_cur)
            dk_cur = lax.ppermute(dk_cur, 'ring', ring_perm)
            dv_cur = lax.ppermute(dv_cur, 'ring', ring_perm)
            if hop_idx < ring_size - 1:
                k_cur = lax.ppermute(k_cur, 'ring', ring_perm)
                v_cur = lax.ppermute(v_cur, 'ring', ring_perm)
        dq_tok = lax.all_to_all(dq_acc.astype(jnp.bfloat16), 'uly', 1, 2, tiled=True)
        dk_tok = lax.all_to_all(dk_cur.astype(jnp.bfloat16), 'uly', 1, 2, tiled=True)
        dv_tok = lax.all_to_all(dv_cur.astype(jnp.bfloat16), 'uly', 1, 2, tiled=True)
        dq_norm = rope_turn(dq_tok.astype(jnp.float32), cos_tab, -sin_tab).reshape(n_batch, n_tok, model_width)
        dk_norm = rope_turn(dk_tok.astype(jnp.float32), cos_tab, -sin_tab).reshape(n_batch, n_tok, model_width)
        d_preq, dg_q = norm_back(dq_norm, pre_q, inv_q, g_q)
        d_prek, dg_k = norm_back(dk_norm, pre_k, inv_k, g_k)
        flat_dq = d_preq.reshape(n_rows, model_width)
        flat_dk = d_prek.reshape(n_rows, model_width)
        flat_dv = dv_tok.reshape(n_rows, model_width)
        dw_q = lax.dot_general(flat_y, flat_dq, ROW_SUM_DIMS, preferred_element_type=jnp.float32)
        dw_k = lax.dot_general(flat_y, flat_dk, ROW_SUM_DIMS, preferred_element_type=jnp.float32)
        dw_v = lax.dot_general(flat_y, flat_dv, ROW_SUM_DIMS, preferred_element_type=jnp.float32)
        db_q = jnp.sum(flat_dq, axis=0, dtype=jnp.float32)
        db_k = jnp.sum(flat_dk, axis=0, dtype=jnp.float32)
        db_v = jnp.sum(flat_dv, axis=0, dtype=jnp.float32)
        grad_rows = lax.dot_general(flat_dq, w_q, BY_TRANSPOSE, preferred_element_type=jnp.float32) + lax.dot_general(flat_dk, w_k, BY_TRANSPOSE, preferred_element_type=jnp.float32) + lax.dot_general(flat_dv, w_v, BY_TRANSPOSE, preferred_element_type=jnp.float32)
        grad_y = grad_rows.astype(jnp.bfloat16).reshape(n_batch, n_tok, model_width)
        grads = lax.psum((dw_q, dw_k, dw_v, dw_o, db_q, db_k, db_v, db_o, dg_q, dg_k), ('dp', 'ring', 'uly'))
        return (grad_y,) + tuple(grads)

    in_specs = (tok_three, tok_three, tok_three, tok_two, tok_two, stat_spec, tok_three, P('dp', None), tok_three, P(('ring', 'uly'), None), whole, whole, whole, whole, whole, whole, whole)
    out_specs = (tok_three, whole, whole, whole, whole, whole, whole, whole, whole, whole, whole)
    return jax.shard_map(device_fn, mesh=mesh, in_specs=in_specs, out_specs=out_specs, check_vma=False)
```

profile of v0, /device:TPU:0, one launch (start us, length us, event | category | flops | bytes accessed | tf_op | source)
XLA Modules:
  0.0 2784.8 jit_solution(367004404073606293)
XLA Ops:
  65.9 15.7 copy.192
  86.9 15.7 copy.196
  110.2 17.2 subtract_convert_fusion
  127.4 20.8 maximum_reduce_fusion.1
  158.6 21.9 maximum_reduce_fusion
  248.2 602.9 %while.36 = (s32[]{:T(128)}, f32[1,4096,3,128]{3,1,2,0:T(8,128)}, f32[1,4096,3,128]{1,3,2,0:T(8,128)}, f32[1,4096,3,128]{1,3,2,0:T(8,128)}, bf16[1,4096,3,128]{3...) while((s32[]{:T(128)}, f32[1,4096,3,128]{3,1,2,0:T(8,128)}, ...), condition=%wide.region_1.0_spmd.clone, body=%wide.region_0.0_spmd.clone.sunk | while | flops 4059758592 | bytes 117986568 | solution.py:59
  486.7 12.0 bitcast_add_fusion.11
  524.6 12.0 bitcast_add_fusion.11
  562.5 12.0 bitcast_add_fusion.11
  600.4 12.0 bitcast_add_fusion.11
  855.2 336.5 %collective-permute-done.3 = bf16[1,4096,3,128]{3,1,2,0:T(8,128)(2,1)} collective-permute-done((bf16[1,4096,3,128]{3,1,2,0:T(8,128)(2,1)}, bf16[1,4096,3,128]{3,1,2,0:T(8,128)(2,1)}, u32[]{:S(2)}, u32[]{:S(2)}) %collective-permute-start.3) | collective-permute-done | bytes 3145760 | tf_op jit(solution)/shard_map/ppermute | solution.py:105
  1191.8 66.3 %collective-permute-done.2 = bf16[1,4096,3,128]{3,1,2,0:T(8,128)(2,1)} collective-permute-done((bf16[1,4096,3,128]{3,1,2,0:T(8,128)(2,1)}, bf16[1,4096,3,128]{3,1,2,0:T(8,128)(2,1)}, u32[]{:S(2)}, u32[]{:S(2)}) %collective-permute-start.2) | collective-permute-done | bytes 3145760 | tf_op jit(solution)/shard_map/ppermute | solution.py:104
  1258.1 646.8 %while.35 = (s32[]{:T(128)}, f32[1,4096,3,128]{3,1,2,0:T(8,128)}, f32[1,4096,3,128]{1,3,2,0:T(8,128)}, f32[1,4096,3,128]{1,3,2,0:T(8,128)}, bf16[1,4096,3,128]{3...) while((s32[]{:T(128)}, f32[1,4096,3,128]{3,1,2,0:T(8,128)}, ...), condition=%wide.region_3.0_spmd, body=%wide.region_2.0_spmd.sunk | while | flops 4056612864 | bytes 92820680 | solution.py:59
  1915.2 20.9 copy.216
  1946.5 34.6 %collective-permute-done.4 = bf16[1,4096,3,128]{3,1,2,0:T(8,128)(2,1)} collective-permute-done((bf16[1,4096,3,128]{3,1,2,0:T(8,128)(2,1)}, bf16[1,4096,3,128]{3,1,2,0:T(8,128)(2,1)}, u32[]{:S(2)}, u32[]{:S(2)}) %collective-permute-start.4) | collective-permute-done | bytes 3145760 | tf_op jit(solution)/shard_map/ppermute | solution.py:101
  2004.3 19.7 copy.217
  2024.0 22.8 collective-permute-done.5
  2058.5 19.9 copy.222
  2078.4 15.5 multiply_subtract_fusion
  2093.9 12.5 pad_maximum_fusion
  2106.4 15.7 copy.218
  2122.1 15.9 copy.223
  2193.5 43.3 %all-reduce = (f32[1536]{0:T(1024)}, f32[1536]{0:T(1024)}, f32[1536]{0:T(1024)}, f32[1536]{0:T(1024)}, f32[1536]{0:T(1024)}, /*index=5*/f32[1536]{0:T(1024)}) all-reduce(f32[1536]{0:T(1024)S(1)} %get-tuple-element.614, f32[1536]{0:T(1024)S(1)} %get-tuple-element.612, ...), channel_id=1, replica_groups=mesh['dp'=4,'ring'=2,'uly'=4] {'dp','ring','uly'}, use_global_device_ids=true, to_apply=%region_11.0 | all-reduce | flops 9216 | bytes 73728 | tf_op jit(solution)/shard_map/psum | solution.py:124
  2260.9 478.5 %all-reduce.4.cloned.1.call-done = (f32[1536,1536]{0,1:T(8,128)}, f32[1536,1536]{0,1:T(8,128)}, f32[1536,1536]{0,1:T(8,128)}, f32[1536,1536]{0,1:T(8,128)}) async-done(((f32[1536,1536]{0,1:T(8,128)}, f32[1536,1536]{0,1:T(8,128)}, f32[1536,1536]{0,1:T(8,128)}, f32[1536,1536]{0,1:T(8,128)}), (f32[1536,1536]{0,1:T(8,128)}, f32[1536,1536]{0,1:T(8,128)}, f32[1536,1536]{0,1:T(8,128)}, ...) | async-done | bytes 37748752 | tf_op jit(solution)/shard_map/psum | solution.py:124
  (389 shorter events, 1528.1 us)
Async XLA Ops:
  7.2 40.0 %copy-start = (bf16[1,1024,1536]{2,1,0:T(8,128)(2,1)S(1)}, bf16[1,1024,1536]{2,1,0:T(8,128)(2,1)}, u32[]{:S(2)}) copy-start(bf16[1,1024,1536]{2,1,0:T(8,128)(2,1)} %param.21) | copy-start | bytes 9437188
  7.2 28.2 %all-to-all-start.2 = ((f32[1,12,1024]{2,0,1:T(1,128)}), f32[1,12,1024]{2,0,1:T(1,128)S(1)}, u32[]{:S(2)}, u32[]{:S(2)}) async-start(f32[1,12,1024]{2,0,1:T(1,128)} %param.26), calls=%async_computation.2 | async-start | bytes 98304 | tf_op jit(solution)/shard_map/all_to_all | solution.py:92
  31.0 16.2 copy-start.24
  42.5 62.6 %all-to-all-start.3 = ((bf16[1,1024,12,128]{1,3,0,2:T(8,128)(2,1)}), bf16[1,1024,12,128]{1,3,0,2:T(8,128)(2,1)}, u32[]{:S(2)}, u32[]{:S(2)}) async-start(bf16[1,1024,12,128]{1,3,0,2:T(8,128)(2,1)} %bitcast.272), calls=%async_computation.3 | async-start | bytes 6291456 | tf_op jit(solution)/shard_map/all_to_all | solution.py:91
  65.9 15.7 copy-start.16
  65.9 15.7 copy-start.20
  105.0 22.3 copy-start.11
  105.1 48.9 %all-to-all-start.4 = ((bf16[1,1024,12,128]{1,3,0,2:T(8,128)(2,1)}), bf16[1,1024,12,128]{1,3,0,2:T(8,128)(2,1)}, u32[]{:S(2)}, u32[]{:S(2)}) async-start(bf16[1,1024,12,128]{1,3,0,2:T(8,128)(2,1)} %bitcast.282), calls=%async_computation.4 | async-start | bytes 6291456 | tf_op jit(solution)/shard_map/all_to_all | solution.py:90
  153.9 41.3 %all-to-all-start.1 = ((bf16[1,1024,12,128]{1,3,0,2:T(8,128)(2,1)}), bf16[1,1024,12,128]{1,3,0,2:T(8,128)(2,1)}, u32[]{:S(2)}, u32[]{:S(2)}) async-start(bf16[1,1024,12,128]{1,3,0,2:T(8,128)(2,1)} %bitcast.283), calls=%async_computation.1 | async-start | bytes 6291456 | tf_op jit(solution)/shard_map/all_to_all | solution.py:89
  195.2 41.5 %all-to-all-start = ((bf16[1,1024,12,128]{1,3,0,2:T(8,128)(2,1)}), bf16[1,1024,12,128]{1,3,0,2:T(8,128)(2,1)}, u32[]{:S(2)}, u32[]{:S(2)}) async-start(bf16[1,1024,12,128]{1,3,0,2:T(8,128)(2,1)} %bitcast.281), calls=%async_computation | async-start | bytes 6291456 | tf_op jit(solution)/shard_map/all_to_all | solution.py:88
  851.1 407.0 %collective-permute-start.1 = (f32[1,4096,3,128]{1,3,2,0:T(8,128)}, f32[1,4096,3,128]{1,3,2,0:T(8,128)}, u32[]{:S(2)}, u32[]{:S(2)}) collective-permute-start(f32[1,4096,3,128]{1,3,2,0:T(8,128)} %get-tuple-element.355), channel_id=1, source_target_pairs={{0,4},{4,0},{1,5},{5,1},{2,6},{6,2},{3,7},{7,3},{8,12},{12,8},{9,1... | collective-permute-start | bytes 18874376 | tf_op jit(solution)/shard_map/ppermute | solution.py:102
  853.1 405.0 %collective-permute-start = (f32[1,4096,3,128]{1,3,2,0:T(8,128)}, f32[1,4096,3,128]{1,3,2,0:T(8,128)}, u32[]{:S(2)}, u32[]{:S(2)}) collective-permute-start(f32[1,4096,3,128]{1,3,2,0:T(8,128)} %get-tuple-element.354), channel_id=1, source_target_pairs={{0,4},{4,0},{1,5},{5,1},{2,6},{6,2},{3,7},{7,3},{8,12},{12,8},{9,1... | collective-permute-start | bytes 18874376 | tf_op jit(solution)/shard_map/ppermute | solution.py:101
  853.2 338.5 %collective-permute-start.3 = (bf16[1,4096,3,128]{3,1,2,0:T(8,128)(2,1)}, bf16[1,4096,3,128]{3,1,2,0:T(8,128)(2,1)}, u32[]{:S(2)}, u32[]{:S(2)}) collective-permute-start(bf16[1,4096,3,128]{3,1,2,0:T(8,128)(2,1)} %get-tuple-element.862), channel_id=1, source_target_pairs={{0,4},{4,0},{1,5},{5,1},{2,6},{6,2},{3,7},{7,3},{8,12},{12,8},{9,1... | collective-permute-start | bytes 9437192 | tf_op jit(solution)/shard_map/ppermute | solution.py:105
  855.2 402.9 %collective-permute-start.2 = (bf16[1,4096,3,128]{3,1,2,0:T(8,128)(2,1)}, bf16[1,4096,3,128]{3,1,2,0:T(8,128)(2,1)}, u32[]{:S(2)}, u32[]{:S(2)}) collective-permute-start(bf16[1,4096,3,128]{3,1,2,0:T(8,128)(2,1)} %get-tuple-element.858), channel_id=1, source_target_pairs={{0,4},{4,0},{1,5},{5,1},{2,6},{6,2},{3,7},{7,3},{8,12},{12,8},{9,1... | collective-permute-start | bytes 9437192 | tf_op jit(solution)/shard_map/ppermute | solution.py:104
  1910.2 71.0 %collective-permute-start.4 = (bf16[1,4096,3,128]{3,1,2,0:T(8,128)(2,1)}, bf16[1,4096,3,128]{3,1,2,0:T(8,128)(2,1)}, u32[]{:S(2)}, u32[]{:S(2)}) collective-permute-start(bf16[1,4096,3,128]{3,1,2,0:T(8,128)(2,1)} %copy.220), channel_id=1, source_target_pairs={{0,4},{4,0},{1,5},{5,1},{2,6},{6,2},{3,7},{7,3},{8,12},{12,8},{9,1... | collective-permute-start | bytes 9437192 | tf_op jit(solution)/shard_map/ppermute | solution.py:101
  1936.0 52.8 %all-to-all-start.6 = ((bf16[1,4096,3,128]{3,2,0,1:T(4,128)(2,1)}), bf16[1,4096,3,128]{3,2,0,1:T(4,128)(2,1)}, u32[]{:S(2)}, u32[]{:S(2)}) async-start(bf16[1,4096,3,128]{3,2,0,1:T(4,128)(2,1)} %copy.216), calls=%async_computation.6 | async-start | bytes 8388608 | tf_op jit(solution)/shard_map/all_to_all | solution.py:106
  1946.3 47.4 %copy-start.13 = (f32[1024,64]{0,1:T(8,128)S(1)}, f32[1024,64]{0,1:T(8,128)}, u32[]{:S(2)}) copy-start(f32[1024,64]{0,1:T(8,128)} %get-tuple-element.633) | copy-start | bytes 786436
  1946.3 48.1 %copy-start.19 = (f32[1,1024]{1,0:T(1,128)S(1)}, f32[1,1024]{1,0:T(1,128)}, u32[]{:S(2)}) copy-start(f32[1,1024]{1,0:T(1,128)} %param.24) | copy-start | bytes 12292
  1946.3 100.5 %collective-permute-start.5 = (bf16[1,4096,3,128]{3,1,2,0:T(8,128)(2,1)}, bf16[1,4096,3,128]{3,1,2,0:T(8,128)(2,1)}, u32[]{:S(2)}, u32[]{:S(2)}) collective-permute-start(bf16[1,4096,3,128]{3,1,2,0:T(8,128)(2,1)} %copy.225), channel_id=1, source_target_pairs={{0,4},{4,0},{1,5},{5,1},{2,6},{6,2},{3,7},{7,3},{8,12},{12,8},{9,1... | collective-permute-start | bytes 9437192 | tf_op jit(solution)/shard_map/ppermute | solution.py:102
  1988.8 64.8 %all-to-all-start.7 = ((bf16[1,4096,3,128]{3,2,0,1:T(4,128)(2,1)}), bf16[1,4096,3,128]{3,2,0,1:T(4,128)(2,1)}, u32[]{:S(2)}, u32[]{:S(2)}) async-start(bf16[1,4096,3,128]{3,2,0,1:T(4,128)(2,1)} %copy.221), calls=%async_computation.7 | async-start | bytes 8388608 | tf_op jit(solution)/shard_map/all_to_all | solution.py:107
  2053.6 93.2 %all-to-all-start.8 = ((bf16[1,4096,3,128]{3,2,0,1:T(4,128)(2,1)}), bf16[1,4096,3,128]{3,2,0,1:T(4,128)(2,1)}, u32[]{:S(2)}, u32[]{:S(2)}) async-start(bf16[1,4096,3,128]{3,2,0,1:T(4,128)(2,1)} %copy.226), calls=%async_computation.8 | async-start | bytes 8388608 | tf_op jit(solution)/shard_map/all_to_all | solution.py:108
  2058.5 19.9 copy-start.12
  2058.5 680.9 %all-reduce.4.cloned.1.call-start = ((), (), s32[]{:S(2)}) async-start(), calls=%async_computation.9 | async-start | bytes 75497472 | tf_op jit(solution)/shard_map/psum | solution.py:124
  2122.1 15.9 copy-start.17
  (48 other events, 358.7 us)
Sparse Core Ops, SparseCore 0:
  2188.7 550.6 all-reduce.3
where the time goes:
time: 2800 us; the launch traced here: 2780 us
  matrix products  1320 us (47%)
  waiting for transfers between devices  960 us (34%)
  local copies, waits for them, and re-layouts  265 us (9%)
  other arithmetic  126 us (4%)
  blocking collectives  50.4 us (2%)
  starting transfers between devices  44.7 us (2%)
    psum x1, waiting for transfers between devices, device_fn(): lax.psum((dw_q, dw_k, dw_v, dw_o, db_q, db_k, db_v, db_o, dg_q, dg_k), ('...  479 us
    dot_general x32, matrix products, blk_body(): jnp.einsum('bhqk,bqhd->bkhd', p_mat.astype(jnp.bfloat16), da_blk, preferr...  380 us
    ppermute x1, waiting for transfers between devices, device_fn(): v_cur = lax.ppermute(v_cur, 'ring', ring_perm)  337 us
    dot_general x32, matrix products, blk_body(): jnp.einsum('bqhd,bkhd->bhqk', q_blk, k_seg, preferred_element_type=jnp.fl...  269 us
    dot_general x32, matrix products, blk_body(): jnp.einsum('bqhd,bkhd->bhqk', da_blk, v_seg, preferred_element_type=jnp.f...  243 us
    dot_general x32, matrix products, blk_body(): jnp.einsum('bhqk,bqhd->bkhd', ds_low, q_blk, preferred_element_type=jnp.f...  227 us
    dot_general x32, matrix products, blk_body(): jnp.einsum('bhqk,bkhd->bqhd', ds_low, k_seg, preferred_element_type=jnp.f...  130 us
    ppermute x1, waiting for transfers between devices, device_fn(): k_cur = lax.ppermute(k_cur, 'ring', ring_perm)  66.3 us
  transfers between devices with their start and end apart: 15, of which 8 were waited for; matrix products, arithmetic and copies ran while one was open for 13% of the time, Pallas kernels for 0%

commit v1 on v0

v1 whole, which is shorter than its diff:
```python
import functools

import jax
import jax.numpy as jnp
from jax import lax
from jax.experimental import pallas as pl
from jax.experimental.pallas import tpu as pltpu
from jax.sharding import PartitionSpec as P


F32 = jnp.float32
BF16 = jnp.bfloat16
LOG2E = 1.4426950408889634
GROUP = ('ring', 'uly')
VMEM_LIMIT = 66 * 1000 * 1000
BY_TRANSPOSE = (((1,), (1,)), ((), ()))
NQ_BLK = 1024
NK_BLK = 512
UNROLL = 2


def split3(col):
    hi = col.astype(BF16)
    rest = col - hi.astype(F32)
    mid = rest.astype(BF16)
    low = (rest - mid.astype(F32)).astype(BF16)
    return hi, mid, low


def ext_cols(col, lane):
    hi, mid, low = (x.astype(F32) for x in split3(col))
    return jnp.where(lane == 0, hi, jnp.where(lane == 1, mid, jnp.where(lane == 2, low, 0.0))).astype(BF16)


def rope_tables(cs, half):
    width = 2 * half
    row = lax.broadcasted_iota(jnp.int32, (width, width), 0)
    col = lax.broadcasted_iota(jnp.int32, (width, width), 1)
    pick_c = jnp.where(row == col // 2, 1.0, 0.0).astype(BF16)
    sign = jnp.where(col % 2 == 0, -1.0, 1.0)
    pick_s = jnp.where(row == half + col // 2, sign, 0.0).astype(BF16)
    pieces = split3(cs)
    cos_t = sum(jnp.dot(x, pick_c, preferred_element_type=F32) for x in pieces)
    sin_t = sum(jnp.dot(x, pick_s, preferred_element_type=F32) for x in pieces)
    return cos_t, sin_t


def swap_pairs(x, lane):
    width = x.shape[-1]
    return jnp.where(lane % 2 == 0, pltpu.roll(x, width - 1, 1), pltpu.roll(x, 1, 1))


def attn_kernel(scale, whole_q, n_qp, *refs):
    in_refs, refs = refs[:n_qp], refs[n_qp:]
    (stat_ref, gain_ref, cs_ref), refs = refs[:3], refs[3:]
    dq_refs, refs = refs[:n_qp], refs[n_qp:]
    dk_ref, dv_ref, qx, dax, kx, vx, qt, dat, kr, dkt, dvt, in_buf, in_sem, cs_buf, cs_sem = refs
    n_part, tok, dim = dq_refs[0].shape
    n_kb = dk_ref.shape[0]
    half = dim // 2
    lane = lax.broadcasted_iota(jnp.int32, (tok, dim), 1)
    sub = lax.broadcasted_iota(jnp.int32, (dim, tok), 0)
    ones = jnp.where(sub < 3, 1.0, 0.0).astype(BF16)
    lse_t = jnp.transpose(stat_ref[0]) * (-1.0 / scale)
    del_t = jnp.transpose(stat_ref[1]) * -1.0
    ivq_t = jnp.transpose(stat_ref[2])
    ivk_t = jnp.transpose(stat_ref[3])
    gain_q = gain_ref[0:1, :]
    gain_k = gain_ref[1:2, :]

    def in_copy(blk):
        src = in_refs[blk // n_part].at[blk % n_part]
        return pltpu.make_async_copy(src, in_buf.at[blk % 2, pl.ds(0, src.shape[0])], in_sem.at[blk % 2])

    def cs_copy(blk):
        return pltpu.make_async_copy(cs_ref.at[blk], cs_buf.at[blk % 2], cs_sem.at[blk % 2])

    def tables(blk, last):
        cs_copy(blk).wait()
        found = rope_tables(cs_buf[blk % 2], half)
        if blk + 2 <= last:
            cs_copy(blk + 2).start()
        return found

    def turned(pre, inv_col, gain, cos_t, sin_t):
        normed = pre.astype(F32) * inv_col * gain
        return (normed * cos_t + swap_pairs(normed, lane) * sin_t).astype(BF16)

    n_qb = n_qp * n_part
    in_copy(0).start()
    cs_copy(0).start()
    cs_copy(1).start()
    for blk in range(n_qp * n_part):
        rows = slice(blk * tok, (blk + 1) * tok)
        cos_t, sin_t = tables(blk, n_qb - 1)
        in_copy(blk).wait()
        if blk + 1 < n_qb:
            in_copy(blk + 1).start()
        slot = blk % 2
        q_blk = turned(in_buf[slot, 0], ivq_t[:, blk:blk + 1], gain_q, cos_t, sin_t)
        da_blk = in_buf[slot, 1]
        qx[rows, :dim] = q_blk
        qx[rows, dim:] = ext_cols(jnp.broadcast_to(lse_t[:, blk:blk + 1], (tok, dim)), lane)
        dax[rows, :dim] = da_blk
        dax[rows, dim:] = ext_cols(jnp.broadcast_to(del_t[:, blk:blk + 1], (tok, dim)), lane)
        qt[:, rows] = jnp.transpose(q_blk)
        dat[:, rows] = jnp.transpose(da_blk)
        if blk < n_kb:
            k_blk = turned(in_buf[slot, 2], ivk_t[:, blk:blk + 1], gain_k, cos_t, sin_t)
            kr[rows, :] = k_blk
            kx[:dim, rows] = jnp.transpose(k_blk)
            kx[dim:, rows] = ones
            vx[:dim, rows] = jnp.transpose(in_buf[slot, 3])
            vx[dim:, rows] = ones
    dkt[...] = jnp.zeros_like(dkt)
    dvt[...] = jnp.zeros_like(dvt)
    q_step, k_step = min(NQ_BLK, tok), NK_BLK
    per_blk = tok // q_step
    n_k = n_kb * tok

    for part in range(n_qp):
        base = part * n_part * tok

        def q_loop(qi, carry, part=part, base=base):
            qs = pl.ds(pl.multiple_of(base + qi * q_step, q_step), q_step)

            def one(j):
                ks = pl.ds(pl.multiple_of(j * k_step, k_step), k_step)
                s_mat = jnp.dot(qx[qs, :], kx[:, ks], preferred_element_type=F32)
                p_mat = jnp.exp2(s_mat * (scale * LOG2E))
                dp_mat = jnp.dot(dax[qs, :], vx[:, ks], preferred_element_type=F32)
                ds_low = (p_mat * dp_mat).astype(BF16)
                p_low = p_mat.astype(BF16)
                dvt[:, ks] += jnp.dot(dat[:, qs], p_low, preferred_element_type=F32)
                dkt[:, ks] += jnp.dot(qt[:, qs], ds_low, preferred_element_type=F32)
                return jnp.dot(ds_low, kr[ks, :], preferred_element_type=F32)

            def k_loop(jj, acc):
                for u in range(UNROLL):
                    acc = acc + one(jj * UNROLL + u)
                return acc

            acc = lax.fori_loop(0, n_k // k_step // UNROLL, k_loop, jnp.zeros((q_step, dim), F32))
            dq_refs[part][qi // per_blk, pl.ds(pl.multiple_of((qi % per_blk) * q_step, q_step), q_step), :] = acc
            return carry

        lax.fori_loop(0, n_part * per_blk, q_loop, 0)

    cs_copy(0).start()
    cs_copy(1).start()
    for blk in range(n_kb):
        rows = slice(blk * tok, (blk + 1) * tok)
        cos_t, sin_t = tables(blk, n_kb - 1)

        def unturned(total):
            low = (total * scale).astype(BF16).astype(F32)
            return low * cos_t - swap_pairs(low, lane) * sin_t

        if whole_q:
            dq_refs[0][blk] = unturned(dq_refs[0][blk])
        dk_ref[blk] = unturned(jnp.transpose(dkt[:, rows]))
        dv_ref[blk] = jnp.transpose(dvt[:, rows]).astype(BF16)


def attn_back(parts, n_kb, stats, gains, cs_all, scale):
    n_qp = len(parts)
    n_part, _, tok, dim = parts[0].shape
    n_q, n_k = n_qp * n_part * tok, n_kb * tok
    vm = pl.BlockSpec(memory_space=pltpu.VMEM)
    far = pl.BlockSpec(memory_space=pltpu.HBM)
    outs = tuple(jax.ShapeDtypeStruct((n_part, tok, dim), F32) for _ in range(n_qp))
    outs += (jax.ShapeDtypeStruct((n_kb, tok, dim), F32), jax.ShapeDtypeStruct((n_kb, tok, dim), BF16))
    return pl.pallas_call(
        functools.partial(attn_kernel, scale, n_q == n_k, n_qp),
        out_shape=outs,
        in_specs=[far] * n_qp + [vm] * 2 + [far],
        out_specs=(vm,) * (n_qp + 2),
        scratch_shapes=[
            pltpu.VMEM((n_q, 2 * dim), BF16), pltpu.VMEM((n_q, 2 * dim), BF16),
            pltpu.VMEM((2 * dim, n_k), BF16), pltpu.VMEM((2 * dim, n_k), BF16),
            pltpu.VMEM((dim, n_q), BF16), pltpu.VMEM((dim, n_q), BF16),
            pltpu.VMEM((n_k, dim), BF16),
            pltpu.VMEM((dim, n_k), F32), pltpu.VMEM((dim, n_k), F32),
            pltpu.VMEM((2, 4, tok, dim), BF16), pltpu.SemaphoreType.DMA((2,)),
            pltpu.VMEM((2, tok, dim), F32), pltpu.SemaphoreType.DMA((2,)),
        ],
        compiler_params=pltpu.CompilerParams(vmem_limit_bytes=VMEM_LIMIT),
        cost_estimate=pl.CostEstimate(flops=n_q * dim, bytes_accessed=n_q, transcendentals=0),
    )(*parts, stats, gains, cs_all)


def finish_kernel(scale, own_ref, got_ref, cs_ref, out_ref):
    tok, dim = own_ref.shape[1:]
    lane = lax.broadcasted_iota(jnp.int32, (tok, dim), 1)
    cos_t, sin_t = rope_tables(cs_ref[0], dim // 2)
    low = ((own_ref[0] + got_ref[0]) * scale).astype(BF16).astype(F32)
    out_ref[0] = low * cos_t - swap_pairs(low, lane) * sin_t


def finish_shared(own, got, cs_all, scale):
    blk = pl.BlockSpec((1,) + own.shape[1:], lambda i: (i, 0, 0))
    return pl.pallas_call(
        functools.partial(finish_kernel, scale), grid=(own.shape[0],),
        out_shape=jax.ShapeDtypeStruct(own.shape, F32),
        in_specs=[blk, blk, blk], out_specs=blk, name='finish_shared',
        cost_estimate=pl.CostEstimate(flops=own.size * 8, bytes_accessed=own.size * 16, transcendentals=0),
    )(own, got, cs_all)


def proj_kernel(n_solo, q_ref, k_ref, dr_ref, gate_ref, attn_ref, y_ref, wo_ref, wv_ref, bv_ref,
                do_ref, solo_ref, shared_ref, del_ref, dbo_ref):
    dim = solo_ref.shape[-1]
    rows, width = dr_ref.shape
    do = (dr_ref[...].astype(F32) * gate_ref[...]).astype(BF16)
    do_ref[...] = do

    @pl.when(pl.program_id(0) == 0)
    def _():
        dbo_ref[...] = jnp.zeros_like(dbo_ref)

    dbo_ref[...] += jnp.sum(do.astype(F32), axis=0, keepdims=True)
    lane = lax.broadcasted_iota(jnp.int32, (rows, dim), 1)
    d_attn = lax.dot_general(do, wo_ref[...], BY_TRANSPOSE, preferred_element_type=F32).astype(BF16)
    v_rows = (jnp.dot(y_ref[...], wv_ref[...], preferred_element_type=F32) + bv_ref[...]).astype(BF16)
    deltas = jnp.zeros((rows, dim), F32)
    for h in range(width // dim):
        cols = slice(h * dim, (h + 1) * dim)
        out = solo_ref.at[h] if h < n_solo else shared_ref.at[h - n_solo]
        out[0] = q_ref[:, cols]
        out[1] = d_attn[:, cols]
        out[2] = k_ref[:, cols]
        out[3] = v_rows[:, cols]
        row = jnp.sum(d_attn[:, cols].astype(F32) * attn_ref[:, cols].astype(F32), axis=1, keepdims=True)
        deltas = jnp.where(lane == h, row, deltas)
    del_ref[...] = jnp.transpose(deltas)[:del_ref.shape[0], :]


def project(pre_q, pre_k, d_resid, gate, attn, flat_y, w_o, w_v, b_v, n_solo, n_shared, dim):
    n_tok, width = d_resid.shape
    rows = 256
    tile = pl.BlockSpec((rows, width), lambda i: (i, 0))
    fixed = lambda shape: pl.BlockSpec(shape, lambda i: (0, 0))
    solo = pl.BlockSpec((n_solo, 4, rows, dim), lambda i: (0, 0, i, 0))
    shared = pl.BlockSpec((n_shared, 4, rows, dim), lambda i: (0, 0, i, 0))
    return pl.pallas_call(
        functools.partial(proj_kernel, n_solo), grid=(n_tok // rows,),
        out_shape=(jax.ShapeDtypeStruct((n_tok, width), BF16), jax.ShapeDtypeStruct((n_solo, 4, n_tok, dim), BF16),
                   jax.ShapeDtypeStruct((n_shared, 4, n_tok, dim), BF16),
                   jax.ShapeDtypeStruct((16, n_tok), F32), jax.ShapeDtypeStruct((1, width), F32)),
        in_specs=[tile, tile, tile, fixed((1, width)), tile, tile, fixed((width, width)), fixed((width, width)), fixed((1, width))],
        out_specs=(tile, solo, shared, pl.BlockSpec((16, rows), lambda i: (0, i)), fixed((1, width))),
        name='project', compiler_params=pltpu.CompilerParams(vmem_limit_bytes=VMEM_LIMIT),
        cost_estimate=pl.CostEstimate(flops=4 * n_tok * width * width, bytes_accessed=12 * n_tok * width * 2, transcendentals=0),
    )(pre_q, pre_k, d_resid, gate, attn, flat_y, w_o, w_v, b_v)


def grad_kernel(solo_ref, shared_ref, *refs):
    w_refs, out_ref = refs[:3], refs[3]
    total = None
    for i, w_ref in enumerate(w_refs):
        rows = jnp.concatenate([solo_ref[h, i] for h in range(solo_ref.shape[0])]
                               + [shared_ref[h, i] for h in range(shared_ref.shape[0])], axis=1)
        term = lax.dot_general(rows, w_ref[...], BY_TRANSPOSE, preferred_element_type=F32)
        total = term if total is None else total + term
    out_ref[...] = total.astype(BF16)


def grad_rows(solo_tok, shared_tok, weights):
    n_solo, _, n_tok, dim = solo_tok.shape
    n_shared = shared_tok.shape[0]
    width = weights[0].shape[0]
    rows = 256
    solo = pl.BlockSpec((n_solo, 3, rows, dim), lambda i: (0, 0, i, 0))
    shared = pl.BlockSpec((n_shared, 3, rows, dim), lambda i: (0, 0, i, 0))
    fixed = pl.BlockSpec((width, width), lambda i: (0, 0))
    return pl.pallas_call(
        grad_kernel, grid=(n_tok // rows,), out_shape=jax.ShapeDtypeStruct((n_tok, width), BF16),
        in_specs=[solo, shared] + [fixed] * 3, out_specs=pl.BlockSpec((rows, width), lambda i: (i, 0)),
        name='grad_rows', compiler_params=pltpu.CompilerParams(vmem_limit_bytes=VMEM_LIMIT),
        cost_estimate=pl.CostEstimate(flops=6 * n_tok * width * width, bytes_accessed=7 * n_tok * width * 2, transcendentals=0),
    )(solo_tok, shared_tok, *weights)


def assemble_kernel(first_ref, second_ref, out_ref):
    out_ref[...] = jnp.transpose(jnp.concatenate([first_ref[0], second_ref[0]], axis=0))


def assemble(full, which, n_solo, n_uly, n_heads, dim):
    width = full.shape[-1]
    half = dim // 2
    base = 3 * which

    def first(h):
        solo = h < n_solo
        return jnp.where(solo, h, h - n_solo), jnp.where(solo, base, base + 2), 0

    def second(h):
        solo = h < n_solo
        return jnp.where(solo, h, h - n_solo + n_uly), jnp.where(solo, base + 1, base + 2), 0

    return pl.pallas_call(
        assemble_kernel, grid=(n_heads,), out_shape=jax.ShapeDtypeStruct((width, width), F32),
        in_specs=[pl.BlockSpec((1, half, width), first), pl.BlockSpec((1, half, width), second)],
        out_specs=pl.BlockSpec((width, dim), lambda h: (0, h)), name='assemble',
        cost_estimate=pl.CostEstimate(flops=0, bytes_accessed=8 * width * width, transcendentals=0),
    )(full, full)


def solution(mesh):
    n_ring, n_uly = mesh.shape['ring'], mesh.shape['uly']
    n_grp = n_ring * n_uly
    ring_swap = [(idx, (idx + 1) % n_ring) for idx in range(n_ring)]
    tok_three = P('dp', GROUP, None)
    tok_two = P('dp', GROUP)
    whole = P()

    def device_fn(y_mod, pre_q, pre_k, inv_q, inv_k, log_sum, attn_out, gate, d_resid, angles, w_q, w_k, w_v, b_v, w_o, g_q, g_k):
        _, n_tok, width = y_mod.shape
        n_heads = log_sum.shape[1]
        dim = width // n_heads
        scale = dim ** -0.5
        n_solo, n_shared = n_grp, n_heads - n_grp
        ring_i, uly_i = lax.axis_index('ring'), lax.axis_index('uly')
        me = ring_i * n_uly + uly_i
        flat_y = y_mod.reshape(n_tok, width)

        def to_mine(arr, axes):
            return lax.all_to_all(arr, axes, 0, 0, tiled=True)

        def own_first(arr):
            flipped = jnp.concatenate([arr[n_uly:], arr[:n_uly]], axis=0)
            return jnp.where(ring_i == 0, arr, flipped)

        cs_own = jnp.concatenate([jnp.cos(angles), jnp.sin(angles)], axis=1)
        cs_all = lax.all_gather(cs_own, GROUP, axis=0)
        stat_own = jnp.concatenate([log_sum[0], inv_q, inv_k], axis=0)
        stat_all = lax.all_gather(stat_own, GROUP, axis=0)

        flat_attn = attn_out.reshape(n_tok, width)
        d_out, solo_s, shared_s, delta_own, db_o = project(
            pre_q.reshape(n_tok, width), pre_k.reshape(n_tok, width), d_resid.reshape(n_tok, width), gate, flat_attn, flat_y,
            w_o, w_v, b_v[None], n_solo, n_shared, dim)
        dw_o = lax.dot_general(flat_attn, d_out, (((0,), (0,)), ((), ())), preferred_element_type=F32)
        delta_all = lax.all_gather(delta_own, GROUP, axis=0)
        shared_s, dw_o, stat_all, delta_all = lax.optimization_barrier((shared_s, dw_o, stat_all, delta_all))
        dw_o = lax.psum(dw_o, ('dp', 'ring', 'uly'))
        shared_in = to_mine(shared_s, 'uly')
        shared_far = lax.ppermute(shared_in[:, :2], 'ring', ring_swap)

        def head_stats(head):
            return (lax.dynamic_index_in_dim(stat_all, head, 1, keepdims=False),
                    lax.dynamic_index_in_dim(delta_all, head, 1, keepdims=False))

        inv_q_all, inv_k_all = stat_all[:, n_heads], stat_all[:, n_heads + 1]
        lse_a, del_a = head_stats(me)
        lse_c, del_c = head_stats(n_solo + uly_i)
        stats_a = jnp.stack([lse_a, del_a, inv_q_all, inv_k_all])
        stats_c = jnp.stack([own_first(x) for x in (lse_c, del_c, inv_q_all, inv_k_all)])
        cs_c = own_first(cs_all)

        def head_gains(head):
            return jnp.concatenate([lax.dynamic_slice_in_dim(g, head * dim, dim, 0)[None] for g in (g_q, g_k)], axis=0)

        gains_a, gains_c = head_gains(me), head_gains(n_solo + uly_i)
        solo_s, shared_far, stats_c, stats_a, cs_c, gains_a, gains_c = lax.optimization_barrier(
            (solo_s, shared_far, stats_c, stats_a, cs_c, gains_a, gains_c))
        solo_in = to_mine(solo_s, GROUP)
        dqc_own, dqc_far, dnk_c, dvc = attn_back((shared_in, shared_far), n_uly, stats_c, gains_c, cs_c, scale)
        dqc_got = lax.ppermute(dqc_far, 'ring', ring_swap)
        dvc_got = lax.ppermute(dvc, 'ring', ring_swap)
        stats_a, late_y, dvc, solo_in = lax.optimization_barrier((stats_a, flat_y, dvc, solo_in))
        y_all = lax.all_gather(late_y, GROUP, axis=0)
        dnq_a, dnk_a, dva = attn_back((solo_in,), n_grp, stats_a, gains_a, cs_all, scale)
        dnq_a, dnk_a, dva, y_all, dqc_got, dvc_got, dw_o = lax.optimization_barrier((dnq_a, dnk_a, dva, y_all, dqc_got, dvc_got, dw_o))
        qa, ka, qc, kc = solo_in[:, 0], solo_in[:, 2], shared_in[:, 0], shared_in[:, 2]
        dnq_c = finish_shared(dqc_own, dqc_got, cs_c, scale)

        def partials(d_norm, proj, inv, gain):
            proj_f = proj.astype(F32)
            return jnp.sum(proj_f * gain * d_norm, axis=-1), jnp.sum(d_norm * proj_f * inv[..., None], axis=(0, 1))

        inv_c = (stats_c[2, :n_uly], stats_c[3, :n_uly])
        mq_a, dgq_a = partials(dnq_a, qa, inv_q_all, gains_a[0])
        mk_a, dgk_a = partials(dnk_a, ka, inv_k_all, gains_a[1])
        mq_c, dgq_c = partials(dnq_c, qc, inv_c[0], gains_c[0])
        mk_c, dgk_c = partials(dnk_c, kc, inv_c[1], gains_c[1])

        def place(own):
            zero = jnp.zeros_like(own)
            return jnp.where(ring_i == 0, jnp.concatenate([own, zero], 0), jnp.concatenate([zero, own], 0))

        mixed = jnp.sum(lax.all_gather(jnp.stack([mq_a + place(mq_c), mk_a + place(mk_c)]), GROUP, axis=0), axis=0) * (1.0 / width)
        mixed, dva_late = lax.optimization_barrier((mixed, dva))
        mixed_c = lax.dynamic_slice_in_dim(mixed, ring_i * n_uly, n_uly, 1)

        def back(d_norm, proj, inv, gain, mix):
            rms = inv[..., None]
            return (rms * gain * d_norm - proj.astype(F32) * rms ** 3 * mix[..., None]).astype(BF16)

        dpq_a = back(dnq_a, qa, inv_q_all, gains_a[0], mixed[0])
        dpk_a = back(dnk_a, ka, inv_k_all, gains_a[1], mixed[1])
        dpq_c = back(dnq_c, qc, inv_c[0], gains_c[0], mixed_c[0])
        dpk_c = back(dnk_c, kc, inv_c[1], gains_c[1], mixed_c[1])

        half = dim // 2

        def cut(arr):
            low, high = arr[..., :half], arr[..., half:]
            return jnp.where(ring_i == 0, low, high), jnp.where(ring_i == 0, high, low)

        (q_keep, q_send), (k_keep, k_send) = cut(dpq_c), cut(dpk_c)
        got = lax.ppermute(jnp.concatenate([q_send, k_send], axis=2), 'ring', ring_swap)

        def block(solo, keep, other):
            cols = jnp.where(ring_i == 0, jnp.concatenate([keep, other], 0), jnp.concatenate([other, keep], 0))
            rows = jnp.concatenate([solo, cols], axis=2)
            dw = lax.dot_general(rows, y_all, (((0, 1), (0, 1)), ((), ())), preferred_element_type=F32)
            return dw, jnp.sum(rows, axis=(0, 1), dtype=F32)

        blocks = [block(dva_late, cut(dvc)[0], cut(dvc_got)[0]), block(dpq_a, q_keep, got[..., :half]), block(dpk_a, k_keep, got[..., half:])]
        vecs = [b[1] for b in blocks] + [dgq_a, dgk_a, dgq_c, dgk_c]
        n_vec = sum(x.shape[0] for x in vecs)
        vec_row = jnp.concatenate(vecs + [jnp.zeros((width - n_vec,), F32)])[None]
        tail_rows = jnp.concatenate([vec_row, db_o, jnp.zeros((6, width), F32)], axis=0)
        n_row = dim + dim * n_shared // n_grp
        mine_v = lax.psum(blocks[0][0], 'dp')
        mine = lax.psum(jnp.concatenate([blocks[1][0], blocks[2][0], tail_rows], axis=0), 'dp')
        solo_ret, shared_ret, got = lax.optimization_barrier((jnp.stack([dpq_a, dpk_a, dva], axis=1), jnp.stack([dpq_c, dpk_c, dvc], axis=1), got))
        solo_tok, shared_tok = to_mine(solo_ret, GROUP), to_mine(shared_ret, 'uly')
        mine_all, solo_tok, shared_tok = lax.optimization_barrier((jnp.concatenate([mine_v, mine], axis=0), solo_tok, shared_tok))
        full = lax.all_gather(mine_all, GROUP, axis=0)

        def whole_dw(i):
            return assemble(full, i, n_solo, n_uly, n_heads, dim)

        def whole_db(i):
            part = full[:, 3 * n_row, i * n_row:(i + 1) * n_row]
            shared = part[:, dim:].reshape(n_ring, n_uly, n_row - dim).transpose(1, 0, 2).reshape(n_shared * dim)
            return jnp.concatenate([part[:, :dim].reshape(n_solo * dim), shared])

        def whole_dg(i):
            start = 3 * n_row
            solo = full[:, 3 * n_row, start + i * dim:start + (i + 1) * dim].reshape(n_solo * dim)
            shared = full[:, 3 * n_row, start + (2 + i) * dim:start + (3 + i) * dim].reshape(n_ring, n_uly, dim)
            return jnp.concatenate([solo, jnp.sum(shared, axis=0).reshape(n_shared * dim)])

        grad_y = grad_rows(solo_tok, shared_tok, (w_q, w_k, w_v)).reshape(y_mod.shape)
        db_o_all = jnp.sum(full[:, 3 * n_row + 1], axis=0)
        return (grad_y, whole_dw(1), whole_dw(2), whole_dw(0), dw_o, whole_db(1), whole_db(2), whole_db(0), db_o_all, whole_dg(0), whole_dg(1))

    in_specs = (tok_three, tok_three, tok_three, tok_two, tok_two, P('dp', None, GROUP), tok_three, P('dp', None), tok_three, P(GROUP, None), whole, whole, whole, whole, whole, whole, whole)
    out_specs = (tok_three, whole, whole, whole, whole, whole, whole, whole, whole, whole, whole)
    return jax.shard_map(device_fn, mesh=mesh, in_specs=in_specs, out_specs=out_specs, check_vma=False)
```

time: 2800 us -> 1020 us (0.36)
  matrix products: 1320 us -> 48.8 us
  waiting for transfers between devices: 960 us -> 379 us
  Pallas kernels: 0 us -> 388 us
  local copies, waits for them, and re-layouts: 265 us -> 46.7 us
  other arithmetic: 126 us -> 70.9 us
    dot_general x169 -> x4, matrix products: 1320 us -> 48.8 us  [the longest x3 38.9 us: block(): lax.dot_general(rows, y_all, (((0, 1), (0, 1)), ((), ())), preferred_elem...]
    ppermute x6 -> x4, waiting for transfers between devices: 460 us -> 30.1 us  [the longest x1 24.6 us: device_fn(): shared_far = lax.ppermute(shared_in[:, :2], 'ring', ring_swap)]
    pallas_call x0 -> x8, Pallas kernels: none -> 388 us  [the longest x2 300 us: attn_back(): pl.pallas_call(functools.partial(attn_kernel, scale, n_q == n_k, n_qp), o...]
    psum x1 -> x2, waiting for transfers between devices: 479 us -> 189 us  [the longest x1 136 us: device_fn(): lax.psum(jnp.concatenate([blocks[1][0], blocks[2][0], tail_rows], axis=0)...]
    all_gather x0 -> x3, waiting for transfers between devices: none -> 106 us  [the longest x1 106 us: device_fn(): full = lax.all_gather(mine_all, GROUP, axis=0)]
    convert_element_type x9 -> x0, local copies, waits for them, and re-layouts: 94.6 us -> none  [the longest x1 20.9 us: device_fn(): dq_acc.astype(jnp.bfloat16)]
    another operation x4 -> x7, other arithmetic: 72.4 us -> 8.04 us  [the longest x1 3.38 us: device_fn(): jnp.stack([dpq_c, dpk_c, dvc], axis=1)]
    psum x1 -> x0, blocking collectives: 43.3 us -> none  [device_fn(): lax.psum((dw_q, dw_k, dw_v, dw_o, db_q, db_k, db_v, db_o, dg_q, dg_k), ('...]
  transfers between devices with their start and end apart: 15 -> 13, of which waited for: 8 -> 8; matrix products, arithmetic and copies ran while one was open for 13% -> 13% of each run, Pallas kernels for 0% -> 34%
where the time goes in v1:
time: 1020 us; the launch traced here: 1010 us
  Pallas kernels  388 us (38%)
  waiting for transfers between devices  379 us (37%)
  other arithmetic  70.9 us (7%)
  matrix products  48.8 us (5%)
  local copies, waits for them, and re-layouts  46.7 us (5%)
  blocking collectives  32.1 us (3%)
  starting transfers between devices  24.4 us (2%)
  between operations  16.2 us (2%)
    pallas_call x2, Pallas kernels, attn_back(): pl.pallas_call(functools.partial(attn_kernel, scale, n_q == n_k, n_qp), o...  300 us
    psum x1, waiting for transfers between devices, device_fn(): lax.psum(jnp.concatenate([blocks[1][0], blocks[2][0], tail_rows], axis=0)...  136 us
    all_gather x1, waiting for transfers between devices, device_fn(): full = lax.all_gather(mine_all, GROUP, axis=0)  106 us
    all_to_all x4, waiting for transfers between devices, to_mine(): return lax.all_to_all(arr, axes, 0, 0, tiled=True)  53.8 us
    psum x1, waiting for transfers between devices, device_fn(): dw_o = lax.psum(dw_o, ('dp', 'ring', 'uly'))  52.7 us
    dot_general x3, matrix products, block(): lax.dot_general(rows, y_all, (((0, 1), (0, 1)), ((), ())), preferred_elem...  38.9 us
    pallas_call x3, Pallas kernels, assemble(): pl.pallas_call(assemble_kernel, grid=(n_heads,), out_shape=jax.ShapeDtype...  37.5 us
    ppermute x1, waiting for transfers between devices, device_fn(): shared_far = lax.ppermute(shared_in[:, :2], 'ring', ring_swap)  24.6 us
  transfers between devices with their start and end apart: 13, of which 8 were waited for; matrix products, arithmetic and copies ran while one was open for 13% of the time, Pallas kernels for 34%

profile of v1, /device:TPU:0, one launch (start us, length us, event | category | flops | bytes accessed | tf_op | source)
XLA Modules:
  0.0 1005.5 jit_solution(7578948926612214813)
XLA Ops:
  13.6 11.3 %all-gather.6 = f32[8,14,1024]{2,1,0:T(8,128)S(1)} all-gather(f32[1,14,1024]{2,1,0:T(8,128)S(1)} %maximum_bitcast_fusion), channel_id=2, replica_groups=mesh['dp'=4,'ring'=2,'uly'=4] {'ring','uly'}, dimensions={0}, use_global_device_ids=true | all-gather | bytes 516096 | tf_op jit(solution)/shard_map/all_gather | solution.py:337
  24.9 20.5 %project.1 = (bf16[1024,1536]{1,0:T(8,128)(2,1)}, bf16[8,4,1024,128]{3,2,1,0:T(8,128)(2,1)}, bf16[4,4,1024,128]{3,2,1,0:T(8,128)(2,1)}, f32[16,1024]{1,0:T(8,128)}, f32[1,1536]{1,0:T(1,128)}) custom-call(bf16[1024,1536]{1,0:T(8,128)(2,1)} %bitcast.238, bf16[1024,1536]{1,0:T(8,128)(2,1)} %bitcast.239, bf16[1024,1536]{1,0:T(8,128)(2,1)} %bitcast.240, ...), custom_call_target="tpu_custom_call" | custom-call | flops 9663676416 | bytes 37748736 | tf_op jit(solution)/shard_map/project/pallas_call | solution.py:245
  45.4 10.9 %all-gather.1 = f32[128,1024]{1,0:T(8,128)S(1)} all-gather(f32[16,1024]{1,0:T(8,128)} %get-tuple-element.55), channel_id=3, replica_groups=mesh['dp'=4,'ring'=2,'uly'=4] {'ring','uly'}, dimensions={0}, use_global_device_ids=true | all-gather | bytes 589824 | tf_op jit(solution)/shard_map/all_gather | solution.py:344
  56.3 9.9 convolution_bitcast_fusion
  73.3 46.1 %all-to-all-done.refs_0_ = bf16[4,4,1024,128]{3,2,1,0:T(8,128)(2,1)} async-done(((bf16[4,4,1024,128]{3,2,1,0:T(8,128)(2,1)}), bf16[4,4,1024,128]{3,2,1,0:T(8,128)(2,1)}, u32[]{:S(2)}, u32[]{:S(2)}) %all-to-all-start) | async-done | bytes 4194336 | tf_op jit(solution)/shard_map/all_to_all | solution.py:328
  145.2 24.6 %collective-permute-done.refs_1_ = bf16[4,2,1024,128]{3,2,1,0:T(8,128)(2,1)} collective-permute-done((bf16[4,2,1024,128]{3,2,1,0:T(8,128)(2,1)}, bf16[4,2,1024,128]{3,2,1,0:T(8,128)(2,1)}, u32[]{:S(2)}, u32[]{:S(2)}) %collective-permute-start) | collective-permute-done | bytes 2097184 | tf_op jit(solution)/shard_map/ppermute | solution.py:348
  175.6 113.5 %shard_map.248 = (f32[4,1024,128]{2,1,0:T(8,128)}, f32[4,1024,128]{2,1,0:T(8,128)}, f32[4,1024,128]{2,1,0:T(8,128)}, bf16[4,1024,128]{2,1,0:T(8,128)(2,1)}) custom-call(bf16[4,4,1024,128]{3,2,1,0:T(8,128)(2,1)} %all-to-all-done.refs_0_, bf16[4,2,1024,128]{3,2,1,0:T(8,128)(2,1)} %collective-permute-done.refs_1_, f32[4,8,1024]{2,1,0:T(8,128)} %pad_maximum_fusion.17.refs_2_, ...), custom_call_target="tpu_custom_call" | custom-call | flops 1048576 | bytes 8192 | tf_op jit(solution)/shard_map/pallas_call | solution.py:173
  296.9 187.0 %shard_map.249 = (f32[8,1024,128]{2,1,0:T(8,128)}, f32[8,1024,128]{2,1,0:T(8,128)}, bf16[8,1024,128]{2,1,0:T(8,128)(2,1)}) custom-call(bf16[8,4,1024,128]{3,2,1,0:T(8,128)(2,1)} %all-to-all-done.1.refs_0_, f32[4,8,1024]{2,1,0:T(8,128)} %pad_maximum_fusion.18.refs_1_, f32[2,128]{1,0:T(2,128)} %copy-done.20, f32[8,1024,128]{2,1,0:T(8,128)} %bitcast.204), custom_call_target="tpu_custom_call" | custom-call | flops 1048576 | bytes 8192 | tf_op jit(solution)/shard_map/pallas_call | solution.py:173
  486.8 52.7 %all-reduce.8.cloned.1.call-done = f32[1536,1536]{0,1:T(8,128)} async-done(((f32[1536,1536]{0,1:T(8,128)}), f32[1536,1536]{0,1:T(8,128)}) %all-reduce.8.cloned.1.call-update) | async-done | bytes 9437200 | tf_op jit(solution)/shard_map/psum | solution.py:346
  545.1 7.5 fusion.13
  556.8 9.8 all-gather.4
  568.9 6.4 fusion.24
  584.8 9.5 fusion.11
  608.1 15.5 %fusion.17 = f32[192,1536]{1,0:T(8,128)} fusion(bf16[8,1024,1536]{2,1,0:T(8,128)(2,1)} %bitcast.200, bf16[8,1024,64]{2,1,0:T(8,128)(2,1)} %maximum_select_fusion.1, bf16[8,1024,128]{2,1,0:T(8,128)(2,1)} %get-tuple-element.81), kind=kOutput, calls=%fused_computation.40 | convolution fusion | flops 4838129664 | bytes 29491200 | tf_op jit(solution)/shard_map/dot_general | solution.py:417
  631.2 10.9 %fusion.18 = f32[192,1536]{1,0:T(8,128)S(1)} fusion(bf16[8,1024,1536]{2,1,0:T(8,128)(2,1)} %bitcast.201, bf16[8,1024,64]{2,1,0:T(8,128)(2,1)S(1)} %maximum_select_fusion.2, bf16[8,1024,128]{2,1,0:T(8,128)(2,1)S(1)} %copy-done.1), kind=kOutput, calls=%fused_computation.41 | convolution fusion | flops 4838129664 | bytes 29491200 | tf_op jit(solution)/shard_map/dot_general | solution.py:417
  654.6 12.5 %fusion.19 = f32[192,1536]{1,0:T(8,128)} fusion(bf16[8,1024,1536]{2,1,0:T(8,128)(2,1)} %bitcast.202, bf16[8,1024,64]{2,1,0:T(8,128)(2,1)} %maximum_select_fusion.3, bf16[8,1024,128]{2,1,0:T(8,128)(2,1)S(1)} %get-tuple-element.147), kind=kOutput, calls=%fused_computation.42 | convolution fusion | flops 4838129664 | bytes 29491200 | tf_op jit(solution)/shard_map/dot_general | solution.py:417
  667.1 6.8 concatenate.169
  673.9 135.9 %all-reduce.10.cloned.1.call-done = (f32[392,1536]{1,0:T(8,128)}, f32[192,1536]{1,0:T(8,128)}) async-done(((f32[392,1536]{1,0:T(8,128)}, f32[192,1536]{1,0:T(8,128)}), (f32[392,1536]{1,0:T(8,128)}, f32[192,1536]{1,0:T(8,128)})) %all-reduce.10.cloned.1.call-update) | async-done | bytes 3588112 | tf_op jit(solution)/shard_map/psum | solution.py:427
  813.9 10.1 %copy.82 = f32[1536,1536]{1,0:T(8,128)} copy(f32[1536,1536]{0,1:T(8,128)} %all-reduce.8.cloned.1.call-done) | data formatting | bytes 18874368
  824.0 23.4 %grad_rows.1 = bf16[1024,1536]{1,0:T(8,128)(2,1)} custom-call(bf16[8,3,1024,128]{3,2,1,0:T(8,128)(2,1)} %all-to-all-done.2.solo_ref, bf16[4,3,1024,128]{3,2,1,0:T(8,128)(2,1)} %all-to-all-done.3.shared_ref, bf16[1536,1536]{1,0:T(8,128)(2,1)} %refs_0_.1, bf16[1536,1536]{1,0:T(8,128)(2,1)} %refs_1_.1, bf16[1536,1536]{1,0:T(8,128)(2,1)} %refs_2_.1), custom_call_target="tpu_custom_call" | custom-call | flops 14495514624 | bytes 22020096 | tf_op jit(solution)/shard_map/grad_rows/pallas_call | solution.py:276
  847.5 105.7 %all-gather.15.cloned.1.call-done = f32[4672,1536]{1,0:T(8,128)} async-done(((f32[584,1536]{1,0:T(8,128)}), f32[4672,1536]{1,0:T(8,128)}) %all-gather.15.cloned.1.call-update) | async-done | bytes 28704784 | tf_op jit(solution)/shard_map/all_gather | solution.py:431
  957.1 12.5 %assemble.5 = f32[1536,1536]{1,0:T(8,128)} custom-call(f32[8,584,1536]{2,1,0:T(8,128)} %bitcast.194, f32[8,584,1536]{2,1,0:T(8,128)} %bitcast.195), custom_call_target="tpu_custom_call" | custom-call | bytes 18874368 | tf_op jit(solution)/shard_map/assemble/pallas_call | solution.py:301
  969.6 12.5 %assemble.4 = f32[1536,1536]{1,0:T(8,128)} custom-call(f32[8,584,1536]{2,1,0:T(8,128)} %bitcast.196, f32[8,584,1536]{2,1,0:T(8,128)} %bitcast.197), custom_call_target="tpu_custom_call" | custom-call | bytes 18874368 | tf_op jit(solution)/shard_map/assemble/pallas_call | solution.py:301
  982.1 12.5 %assemble.3 = f32[1536,1536]{1,0:T(8,128)} custom-call(f32[8,584,1536]{2,1,0:T(8,128)} %bitcast.198, f32[8,584,1536]{2,1,0:T(8,128)} %bitcast.199), custom_call_target="tpu_custom_call" | custom-call | bytes 18874368 | tf_op jit(solution)/shard_map/assemble/pallas_call | solution.py:301
  (153 shorter events, 121.0 us)
Async XLA Ops:
  8.0 116.7 %all-gather.11.cloned.1.call-start = ((), (), s32[]{:S(2)}) async-start(), calls=%async_computation.5 | async-start | bytes 4718592 | tf_op jit(solution)/shard_map/all_gather | solution.py:335
  66.3 53.1 %all-to-all-start = ((bf16[4,4,1024,128]{3,2,1,0:T(8,128)(2,1)}), bf16[4,4,1024,128]{3,2,1,0:T(8,128)(2,1)}, u32[]{:S(2)}, u32[]{:S(2)}) async-start(bf16[4,4,1024,128]{3,2,1,0:T(8,128)(2,1)} %get-tuple-element.56), calls=%async_computation | async-start | bytes 8388608 | tf_op jit(solution)/shard_map/all_to_all | solution.py:328
  73.2 471.9 %copy-start.15 = (f32[8,1024]{1,0:T(8,128)}, f32[8,1024]{1,0:T(8,128)S(1)}, u32[]{:S(2)}) copy-start(f32[8,1024]{1,0:T(8,128)S(1)} %get-tuple-element.164) | copy-start | bytes 98308
  122.4 47.4 %collective-permute-start = (bf16[4,2,1024,128]{3,2,1,0:T(8,128)(2,1)}, bf16[4,2,1024,128]{3,2,1,0:T(8,128)(2,1)}, u32[]{:S(2)}, u32[]{:S(2)}) collective-permute-start(bf16[4,2,1024,128]{3,2,1,0:T(8,128)(2,1)} %slice.222), channel_id=1, source_target_pairs={{0,4},{4,0},{1,5},{5,1},{2,6},{6,2},{3,7},{7,3},{8,12},{12,8},{9,1... | collective-permute-start | bytes 6291464 | tf_op jit(solution)/shard_map/ppermute | solution.py:348
  123.3 173.6 %copy-start.20 = (f32[2,128]{1,0:T(2,128)}, f32[2,128]{1,0:T(2,128)S(1)}, u32[]{:S(2)}) copy-start(f32[2,128]{1,0:T(2,128)S(1)} %pad_maximum_fusion.25.refs_2_) | copy-start | bytes 3076
  169.8 124.3 %all-to-all-start.1 = ((bf16[8,4,1024,128]{3,2,1,0:T(8,128)(2,1)}), bf16[8,4,1024,128]{3,2,1,0:T(8,128)(2,1)}, u32[]{:S(2)}, u32[]{:S(2)}) async-start(bf16[8,4,1024,128]{3,2,1,0:T(8,128)(2,1)} %get-tuple-element.65), calls=%async_computation.1 | async-start | bytes 16777216 | tf_op jit(solution)/shard_map/all_to_all | solution.py:328
  174.8 364.7 %all-reduce.8.cloned.1.call-start = ((), (), s32[]{:S(2)}) async-start(), calls=%async_computation.4 | async-start | bytes 18874368 | tf_op jit(solution)/shard_map/psum | solution.py:346
  175.3 364.1 %all-gather.13.cloned.1.call-start = ((), (), s32[]{:S(2)}) async-start(), calls=%async_computation.6 | async-start | bytes 28311552 | tf_op jit(solution)/shard_map/all_gather | solution.py:372
  289.2 7.6 copy-start.19
  289.2 7.6 copy-start.14
  294.1 245.4 %collective-permute-start.1 = (f32[4,1024,128]{2,1,0:T(8,128)}, f32[4,1024,128]{2,1,0:T(8,128)}, u32[]{:S(2)}, u32[]{:S(2)}) collective-permute-start(f32[4,1024,128]{2,1,0:T(8,128)} %get-tuple-element.73), channel_id=1, source_target_pairs={{0,4},{4,0},{1,5},{5,1},{2,6},{6,2},{3,7},{7,3},{8,12},{12,8},{9,1... | collective-permute-start | bytes 6291464 | tf_op jit(solution)/shard_map/ppermute | solution.py:369
  295.3 244.1 %collective-permute-start.2 = (bf16[4,1024,128]{2,1,0:T(8,128)(2,1)}, bf16[4,1024,128]{2,1,0:T(8,128)(2,1)}, u32[]{:S(2)}, u32[]{:S(2)}) collective-permute-start(bf16[4,1024,128]{2,1,0:T(8,128)(2,1)} %get-tuple-element.82), channel_id=1, source_target_pairs={{0,4},{4,0},{1,5},{5,1},{2,6},{6,2},{3,7},{7,3},{8,12},{12,8},{9,1... | collective-permute-start | bytes 3145736 | tf_op jit(solution)/shard_map/ppermute | solution.py:370
  545.1 7.6 copy-start.2
  545.1 7.6 copy-start.10
  577.6 25.6 %collective-permute-start.3 = (bf16[4,1024,128]{2,1,0:T(8,128)(2,1)S(1)}, bf16[4,1024,128]{2,1,0:T(8,128)(2,1)}, u32[]{:S(2)}, u32[]{:S(2)}) collective-permute-start(bf16[4,1024,128]{2,1,0:T(8,128)(2,1)S(1)} %pad_maximum_fusion.15), channel_id=1, source_target_pairs={{0,4},{4,0},{1,5},{5,1},{2,6},{6,2},{3,7},{7,3},{8,12},{12,8},{9,1... | collective-permute-start | bytes 3145736 | tf_op jit(solution)/shard_map/ppermute | solution.py:412
  579.2 5.6 copy-start.9
  584.8 9.6 copy-start.3
  603.2 41.8 %all-to-all-start.3 = ((bf16[4,3,1024,128]{3,2,1,0:T(8,128)(2,1)}), bf16[4,3,1024,128]{3,2,1,0:T(8,128)(2,1)}, u32[]{:S(2)}, u32[]{:S(2)}) async-start(bf16[4,3,1024,128]{3,2,1,0:T(8,128)(2,1)} %pad_maximum_fusion.5), calls=%async_computation.3 | async-start | bytes 6291456 | tf_op jit(solution)/shard_map/all_to_all | solution.py:328
  608.1 15.5 %copy-start.4 = (bf16[8,1024,128]{2,1,0:T(8,128)(2,1)S(1)}, bf16[8,1024,128]{2,1,0:T(8,128)(2,1)}, u32[]{:S(2)}) copy-start(bf16[8,1024,128]{2,1,0:T(8,128)(2,1)} %get-tuple-element.81) | copy-start | bytes 6291460
  608.1 15.5 %copy-start.6 = (bf16[8,1024,64]{2,1,0:T(8,128)(2,1)S(1)}, bf16[8,1024,64]{2,1,0:T(8,128)(2,1)}, u32[]{:S(2)}) copy-start(bf16[8,1024,64]{2,1,0:T(8,128)(2,1)} %maximum_select_fusion.1) | copy-start | bytes 3145732
  645.0 168.9 %all-to-all-start.2 = ((bf16[8,3,1024,128]{3,2,1,0:T(8,128)(2,1)}), bf16[8,3,1024,128]{3,2,1,0:T(8,128)(2,1)}, u32[]{:S(2)}, u32[]{:S(2)}) async-start(bf16[8,3,1024,128]{3,2,1,0:T(8,128)(2,1)} %pad_maximum_fusion), calls=%async_computation.2 | async-start | bytes 12582912 | tf_op jit(solution)/shard_map/all_to_all | solution.py:328
  649.8 160.0 %all-reduce.10.cloned.1.call-start = ((), (), s32[]{:S(2)}) async-start(), calls=%async_computation.8 | async-start | bytes 7176192 | tf_op jit(solution)/shard_map/psum | solution.py:427
  654.6 12.5 %copy-start.21 = (f32[1,1536]{1,0:T(1,128)S(1)}, f32[1,1536]{1,0:T(1,128)}, u32[]{:S(2)}) copy-start(f32[1,1536]{1,0:T(1,128)} %get-tuple-element.86) | copy-start | bytes 18436
  673.9 279.3 %all-gather.15.cloned.1.call-start = ((), (), s32[]{:S(2)}) async-start(), calls=%async_computation.7 | async-start | bytes 32292864 | tf_op jit(solution)/shard_map/all_gather | solution.py:431
  (11 other events, 31.7 us)
Sparse Core Ops, SparseCore 0:
  11.3 39.2 all-gather.10
  294.2 177.7 all-gather.12
  814.0 139.1 all-gather.14
Sparse Core Ops, SparseCore 1:
  181.6 357.8 all-reduce.7
  674.0 135.8 all-reduce.9
